TPU v7x, 8 devices: a whole 2x2x1 slice. The times are simulated.
8 devices in a mesh: dp: 1 (over z), tp: 2 (over y), cp: 4 (over x, core).
Axes of the slice: x: 2, y: 2, z: 1, core: 2. Of those that a mesh axis runs over, the one named last changes fastest.
Arguments:
- hidden: bfloat16 [1024, 6144], P(('dp', 'cp'))
- seg_ids: int32 [1024], P(('dp', 'cp'))
- w_q: bfloat16 [6144, 6144], P(None, 'tp')
- b_q: bfloat16 [6144], P('tp')
- w_kv: bfloat16 [6144, 256], replicated
- b_kv: bfloat16 [256], replicated
- w_o: bfloat16 [6144, 6144], P('tp')
- b_o: bfloat16 [6144], replicated
- ln_gain: bfloat16 [6144], replicated
- ln_bias: bfloat16 [6144], replicated
Outputs:
- output 1: bfloat16 [1024, 6144], P(('dp', 'cp'))
- output 2: bfloat16 [1024, 128], P(('dp', 'cp'))
- output 3: bfloat16 [1024, 128], P(('dp', 'cp'))
All inputs are finite; a program needn't handle non-finite values.
Results may differ from a plain program's by a relative error of at most 0.0118747.
Values are sent between devices in bfloat16 or wider.
A program may use at most 1 GiB of HBM per device.

v0:
```python
import functools

import jax
import jax.numpy as jnp
from jax import lax
from jax.experimental import pallas as pl
from jax.experimental.pallas import tpu as pltpu
from jax.sharding import PartitionSpec as P

HEAD_DIM = 128
LN_EPS = 1e-5
EXP2_SCALE = HEAD_DIM ** -0.5 * 1.4426950408889634
MESH = pl.DeviceIdType.MESH

CHUNKS = (128, 128)
HALF = 128
TILE_K = 3072
TILE_N = 512
AHEAD = 3
SLOTS = 9
LN_ROWS = 32


def block_kernel(n_cp, hid_hbm, seg_hbm, wq_hbm, bq_hbm, wkv_hbm, bkv_hbm, wo_hbm, bo_hbm, gain_hbm, bias_hbm,
                 y_ref, k_ref, v_ref,
                 normed, wkv, wbuf, kv_all, seg_all, below, mask, qbuf, obuf, send0, send1, recv0, recv1,
                 bq_raw, bkv_raw, bo_raw, gain_raw, bias_raw, bq, bkv, bo, gain, bias,
                 hid_sem, wkv_sem, small_sem, w_sem, kv_send, kv_recv, seg_send, seg_recv, tp_send, tp_recv):
    my = lax.axis_index('cp')
    partner = 1 - lax.axis_index('tp')
    tok, d_model = y_ref.shape
    q_width = qbuf.shape[1]
    n_chunk = len(CHUNKS)
    n_half = tok // HALF
    send, recv = (send0, send1), (recv0, recv1)
    q_tiles = q_width // TILE_N
    k_halves = d_model // TILE_K
    o_tiles = d_model // TILE_N
    q_items = q_tiles * k_halves
    items = q_items + o_tiles
    total = n_chunk * items
    f32, bf16 = jnp.float32, jnp.bfloat16

    def hid_copy(i):
        rows = pl.ds(i * LN_ROWS, LN_ROWS)
        return pltpu.make_async_copy(hid_hbm.at[rows, :], y_ref.at[rows, :], hid_sem.at[i])

    def w_issue(g):
        slot = lax.rem(g, SLOTS)
        item = lax.rem(g, items)

        @pl.when(item < q_items)
        def _():
            col = pl.multiple_of(lax.div(item, k_halves) * TILE_N, TILE_N)
            row = pl.multiple_of(lax.rem(item, k_halves) * TILE_K, TILE_K)
            pltpu.make_async_copy(wq_hbm.at[pl.ds(row, TILE_K), pl.ds(col, TILE_N)], wbuf.at[slot], w_sem.at[slot]).start()

        @pl.when(item >= q_items)
        def _():
            col = pl.multiple_of((item - q_items) * TILE_N, TILE_N)
            pltpu.make_async_copy(wo_hbm.at[:, pl.ds(col, TILE_N)], wbuf.at[slot], w_sem.at[slot]).start()

    def w_wait(g):
        slot = lax.rem(g, SLOTS)
        pltpu.make_async_copy(wo_hbm.at[:, pl.ds(0, TILE_N)], wbuf.at[slot], w_sem.at[slot]).wait()
        return slot

    def w_next(g):
        @pl.when(g + SLOTS < total)
        def _():
            w_issue(g + SLOTS)

    n_ln = tok // LN_ROWS
    ln_half = n_ln // n_half
    small = [pltpu.make_async_copy(src, dst, small_sem.at[i]) for i, (src, dst) in enumerate((
        (gain_hbm, gain_raw), (bias_hbm, bias_raw), (bkv_hbm, bkv_raw), (bq_hbm, bq_raw), (bo_hbm, bo_raw), (seg_hbm, seg_all.at[my])))]
    wkv_copy = pltpu.make_async_copy(wkv_hbm, wkv, wkv_sem)
    hid_copy(0).start()
    for copy in small:
        copy.start()
    for i in range(1, n_ln):
        hid_copy(i).start()

    barrier = pltpu.get_barrier_semaphore()
    for step in range(1, n_cp):
        pl.semaphore_signal(barrier, inc=1, device_id={'cp': lax.rem(my + step, n_cp)}, device_id_type=MESH)
    pl.semaphore_signal(barrier, inc=1, device_id={'tp': partner}, device_id_type=MESH)

    with jax.named_scope("hid"):
        hid_copy(0).wait()
        wkv_copy.start()
        for i in range(1, n_ln):
            hid_copy(i).wait()
            if i >= n_ln - AHEAD:
                w_issue(jnp.int32(i - n_ln + AHEAD))

    with jax.named_scope("small"):
        for copy in small:
            copy.wait()
    gain[...] = gain_raw[...].astype(f32)
    bias[...] = bias_raw[...].astype(f32)
    bkv[...] = bkv_raw[...].astype(f32)
    bq[...] = bq_raw[...].astype(f32)
    bo[...] = bo_raw[...].astype(f32)

    def ln_block(i, carry):
        @pl.when(i < (SLOTS - AHEAD) // 2)
        def _():
            for more in range(2):
                w_issue(i * 2 + more + AHEAD)

        rows = pl.ds(pl.multiple_of(i * LN_ROWS, LN_ROWS), LN_ROWS)
        n_col = d_model // 128

        def load(j):
            return y_ref[rows, j * 128:(j + 1) * 128].astype(f32)

        accs = [load(j) for j in range(4)]
        for j in range(4, n_col):
            accs[j % 4] = accs[j % 4] + load(j)
        mean = jnp.sum((accs[0] + accs[1]) + (accs[2] + accs[3]), axis=-1, keepdims=True) * (1.0 / d_model)
        mean = jnp.broadcast_to(mean, (LN_ROWS, 128))
        accs = [None] * 4
        for j in range(n_col):
            cen = load(j) - mean
            accs[j % 4] = cen * cen if accs[j % 4] is None else accs[j % 4] + cen * cen
        var = jnp.sum((accs[0] + accs[1]) + (accs[2] + accs[3]), axis=-1, keepdims=True) * (1.0 / d_model)
        rstd = jnp.broadcast_to(lax.rsqrt(var + LN_EPS), (LN_ROWS, 128))
        for j in range(n_col):
            out = (load(j) - mean) * rstd * gain[j:j + 1, :] + bias[j:j + 1, :]
            normed[rows, j * 128:(j + 1) * 128] = out.astype(bf16)
        return carry

    def kv_copy(src, h, dst):
        return pltpu.make_async_remote_copy(src_ref=kv_all.at[src, h], dst_ref=kv_all.at[src, h],
                                            send_sem=kv_send.at[dst, h], recv_sem=kv_recv.at[src, h],
                                            device_id={'cp': dst}, device_id_type=MESH)

    def seg_copy(src, dst):
        return pltpu.make_async_remote_copy(src_ref=seg_all.at[src], dst_ref=seg_all.at[src], send_sem=seg_send.at[dst],
                                            recv_sem=seg_recv.at[src], device_id={'cp': dst}, device_id_type=MESH)

    def late(dst):
        return (dst == n_cp - 1) & (my < n_cp // 2)

    def kv_half(h):
        with jax.named_scope("ln"):
            lax.fori_loop(h * ln_half, (h + 1) * ln_half, ln_block, 0)
        rows = pl.ds(h * HALF, HALF)
        if h == 0:
            wkv_copy.wait()
        with jax.named_scope("kvdot"):
            mid = d_model // 2
            low = jnp.dot(normed[rows, :mid], wkv[:mid, :], preferred_element_type=f32)
            high = jnp.dot(normed[rows, mid:], wkv[mid:, :], preferred_element_type=f32)
            k_own = ((low[:, :HEAD_DIM] + bkv[0:1, :]) + high[:, :HEAD_DIM]).astype(bf16)
            v_own = ((low[:, HEAD_DIM:] + bkv[1:2, :]) + high[:, HEAD_DIM:]).astype(bf16)
            kv_all[my, h, 0] = k_own
            kv_all[my, h, 1] = v_own.astype(f32).T.astype(bf16)
            k_ref[rows, :] = k_own
            v_ref[rows, :] = v_own
        if h == 0:
            with jax.named_scope("barrier"):
                pl.semaphore_wait(barrier, n_cp)
            for dst in range(1, n_cp):
                @pl.when(my < dst)
                def _():
                    seg_copy(my, dst).start()

        for dst in range(1, n_cp):
            @pl.when((my < dst) & jnp.logical_not(late(dst)))
            def _():
                kv_copy(my, h, dst).start()

    kv_half(0)

    @pl.when(my < n_cp)
    def _():
        for h in range(1, n_half):
            kv_half(h)

    def tile_copy(c, n):
        return pltpu.make_async_remote_copy(src_ref=send[c].at[n], dst_ref=recv[c].at[n], send_sem=tp_send.at[c, n],
                                            recv_sem=tp_recv.at[c, n], device_id={'tp': partner}, device_id_type=MESH)

    def chunk(c):
        base = c * items
        n_row = CHUNKS[c]
        first = sum(CHUNKS[:c])
        rows = slice(first, first + n_row)

        def q_wait(j):
            return [w_wait(base + j * k_halves + half) for half in range(k_halves)]

        def q_next(j):
            for half in range(k_halves):
                w_next(base + j * k_halves + half)

        def q_dot(j, slots):
            acc = None
            step = TILE_K // 2
            for half in range(k_halves):
                for n in range(2):
                    k0 = half * TILE_K + n * step
                    part = jnp.dot(normed[rows, k0:k0 + step], wbuf[slots[half], n * step:(n + 1) * step, :], preferred_element_type=f32)
                    acc = part if acc is None else acc + part
            return acc

        def q_store(j, acc):
            for i in range(TILE_N // 128):
                cols = pl.ds(pl.multiple_of(j * TILE_N + i * 128, 128), 128)
                row = j * (TILE_N // 128) + i
                qbuf[:, cols] = (acc[:, i * 128:(i + 1) * 128] + bq[pl.ds(row, 1), :]).astype(bf16)

        def q_tile(j, carry):
            with jax.named_scope("qtile"):
                q_store(j, q_dot(j, q_wait(j)))
                q_next(j)
            return carry

        own_keys = first + n_row

        def make_mask():
            if c == 0:
                for src in range(n_cp - 1):
                    @pl.when(src < my)
                    def _():
                        seg_copy(src, src).wait_recv()

            seg_q = jnp.broadcast_to(seg_all[my, c:c + 1, :].astype(f32), (128, 128)).T
            below[...] = jnp.zeros((128, 128), f32)
            for b in range(n_cp * tok // 128):
                src, part = b * 128 // tok, b % (tok // 128)

                @pl.when(b * 128 < my * tok + own_keys)
                def _():
                    below[...] += jnp.where(seg_all[src, part:part + 1, :].astype(f32) < seg_q, 1.0, 0.0)

            prompt = jnp.broadcast_to(jnp.sum(below[...], axis=1, keepdims=True), (128, 128)).T
            key = lax.broadcasted_iota(jnp.int32, (128, 128), 0)
            q_pos = my * tok + first + lax.broadcasted_iota(jnp.int32, (128, 128), 1)
            for b in range(n_cp * tok // 128):
                src, part = b * 128 // tok, b % (tok // 128)

                @pl.when(b * 128 < my * tok + own_keys)
                def _():
                    k_pos = key + b * 128
                    seen = (k_pos.astype(f32) >= prompt) & (k_pos <= q_pos)
                    mask[b * 128:(b + 1) * 128, :] = jnp.where(seen, 0.0, -jnp.inf)

        def heads(j, nb, beside=None):
            cols = pl.ds(pl.multiple_of(j * TILE_N, TILE_N), TILE_N)
            n_head = TILE_N // HEAD_DIM
            keys = nb * tok + own_keys
            parts = [kv_all.at[b * 128 // tok, b % (tok // 128)] for b in range(keys // 128)]
            k_blk = jnp.concatenate([part[0] for part in parts], axis=0)
            v_t = jnp.concatenate([part[1] for part in parts], axis=1)
            q_cols = qbuf[:, cols]
            q_rows = jnp.concatenate([q_cols[:, i * HEAD_DIM:(i + 1) * HEAD_DIM] for i in range(n_head)], axis=0)
            s = lax.dot_general(k_blk, q_rows, (((1,), (1,)), ((), ())), preferred_element_type=f32)
            other = beside() if beside else None
            s = s + jnp.concatenate([mask[:keys, :]] * n_head, axis=1)
            p_wts = jnp.exp2((s - jnp.max(s, axis=0, keepdims=True)) * EXP2_SCALE)
            l_sum = jnp.sum(p_wts, axis=0, keepdims=True)
            o = jnp.dot(v_t, p_wts.astype(bf16), preferred_element_type=f32) / l_sum
            obuf[:, cols] = jnp.concatenate([o[:, i * HEAD_DIM:(i + 1) * HEAD_DIM].T for i in range(n_head)], axis=1).astype(bf16)
            return other

        def attend(j, carry):
            for nb in range(n_cp):
                @pl.when(my == nb)
                def _():
                    with jax.named_scope("attn"):
                        heads(j, nb)
            return carry

        def both(j, carry):
            slots = q_wait(j)
            for nb in range(n_cp):
                @pl.when(my == nb)
                def _():
                    with jax.named_scope("both"):
                        q_store(j, heads(j - lag, nb, lambda: q_dot(j, slots)))
            q_next(j)
            return carry

        lag = jnp.where(my < n_cp // 2, 1, 2)
        q_tile(0, 0)
        lax.fori_loop(1, lag, q_tile, 0)
        with jax.named_scope("mask"):
            make_mask()
        if c == 0:
            @pl.when(late(n_cp - 1))
            def _():
                for h in range(n_half):
                    kv_copy(my, h, n_cp - 1).start()

        if c == 0:
            with jax.named_scope("kvwait"):
                for src in range(n_cp - 1):
                    @pl.when(src < my)
                    def _():
                        for h in range(n_half):
                            kv_copy(src, h, src).wait_recv()
        if c == 0:
            lax.fori_loop(lag, q_tiles, both, 0)
        else:
            def turn(j, carry):
                return attend(j - lag, q_tile(j, carry))

            lax.fori_loop(lag, q_tiles, turn, 0)
        lax.fori_loop(q_tiles - lag, q_tiles, attend, 0)

        def o_tile(n, carry):
            with jax.named_scope("otile"):
                g = base + q_items + n
                slot = w_wait(g)
                send[c][n] = jnp.dot(obuf[:n_row, :], wbuf[slot], preferred_element_type=f32).astype(bf16)
                tile_copy(c, n).start()
                w_next(g)
            return carry

        lax.fori_loop(0, o_tiles, o_tile, 0)

    for c in range(n_chunk):
        chunk(c)

    for dst in range(1, n_cp):
        @pl.when(my < dst)
        def _():
            seg_copy(my, dst).wait_send()
            for h in range(n_half):
                kv_copy(my, h, dst).wait_send()

    for c in range(n_chunk):
        first = sum(CHUNKS[:c])
        rows = slice(first, first + CHUNKS[c])

        def finish(n, carry):
            copy = tile_copy(c, n)
            copy.wait_recv()
            copy.wait_send()
            for i in range(TILE_N // 128):
                cols = pl.ds(pl.multiple_of(n * TILE_N + i * 128, 128), 128)
                part = slice(i * 128, (i + 1) * 128)
                both = send[c][n, :, part].astype(f32) + recv[c][n, :, part].astype(f32)
                y_ref[rows, cols] = (y_ref[rows, cols].astype(f32) + both + bo[pl.ds(n * (TILE_N // 128) + i, 1), :]).astype(bf16)
            return carry

        with jax.named_scope("finish"):
            lax.fori_loop(0, o_tiles, finish, 0)


def close_kernel(y_ref, k_ref, v_ref, y_hbm, k_hbm, v_hbm, sem):
    rows = y_ref.shape[0] // 8
    copies = [pltpu.make_async_copy(k_ref, k_hbm, sem.at[8]), pltpu.make_async_copy(v_ref, v_hbm, sem.at[9])]
    copies += [pltpu.make_async_copy(y_ref.at[pl.ds(i * rows, rows), :], y_hbm.at[pl.ds(i * rows, rows), :], sem.at[i]) for i in range(8)]
    for copy in copies:
        copy.start()
    for copy in copies:
        copy.wait()


def solution(mesh):
    n_cp = mesh.shape['cp']

    def local_block(hidden, seg_ids, w_q, b_q, w_kv, b_kv, w_o, b_o, ln_gain, ln_bias):
        tok, d_model = hidden.shape
        q_width = w_q.shape[1]
        o_tiles = d_model // TILE_N
        vmem = pl.BlockSpec(memory_space=pltpu.VMEM)
        hbm = pl.BlockSpec(memory_space=pltpu.HBM)
        bf16, f32 = jnp.bfloat16, jnp.float32
        dma = pltpu.SemaphoreType.DMA
        flops = 2 * tok * d_model * (2 * q_width + 256)
        args = (hidden, seg_ids.reshape(-1, 128), w_q, b_q.reshape(-1, 128), w_kv, b_kv.reshape(-1, 128), w_o,
                b_o.reshape(-1, 128), ln_gain.reshape(-1, 128), ln_bias.reshape(-1, 128))
        args = tuple(pltpu.with_memory_space_constraint(a, pltpu.HBM) for a in args)
        rows = [q_width // 128, 2, d_model // 128, d_model // 128, d_model // 128]
        y, k, v = pl.pallas_call(
            functools.partial(block_kernel, n_cp),
            out_shape=(pltpu.VMEM((tok, d_model), bf16), pltpu.VMEM((tok, HEAD_DIM), bf16), pltpu.VMEM((tok, HEAD_DIM), bf16)),
            in_specs=[hbm] * len(args),
            out_specs=(vmem, vmem, vmem),
            scratch_shapes=[
                pltpu.VMEM((tok, d_model), bf16),
                pltpu.VMEM((d_model, 2 * HEAD_DIM), bf16),
                pltpu.VMEM((SLOTS, TILE_K, TILE_N), bf16),
                pltpu.VMEM((n_cp, tok // HALF, 2, HALF, HEAD_DIM), bf16),
                pltpu.VMEM((n_cp, tok // 128, 128), jnp.int32),
                pltpu.VMEM((128, 128), f32),
                pltpu.VMEM((n_cp * tok, 128), f32),
                pltpu.VMEM((max(CHUNKS), q_width), bf16),
                pltpu.VMEM((max(CHUNKS), q_width), bf16),
                *[pltpu.VMEM((o_tiles, r, TILE_N), bf16) for r in CHUNKS * 2],
                *[pltpu.VMEM((r, 128), bf16) for r in rows],
                *[pltpu.VMEM((r, 128), f32) for r in rows],
                dma((tok // LN_ROWS,)), dma, dma((6,)), dma((SLOTS,)),
                dma((n_cp, tok // HALF)), dma((n_cp, tok // HALF)), dma((n_cp,)), dma((n_cp,)),
                dma((len(CHUNKS), o_tiles)), dma((len(CHUNKS), o_tiles)),
            ],
            compiler_params=pltpu.CompilerParams(collective_id=0, has_side_effects=True, vmem_limit_bytes=56 * 1024 * 1024),
            cost_estimate=pl.CostEstimate(flops=flops, bytes_accessed=2 * 4 * d_model * q_width, transcendentals=0),
        )(*args)
        return pl.pallas_call(
            close_kernel,
            out_shape=tuple(jax.ShapeDtypeStruct(a.shape, bf16) for a in (y, k, v)),
            in_specs=[vmem] * 3,
            out_specs=(hbm,) * 3,
            scratch_shapes=[dma((10,))],
            cost_estimate=pl.CostEstimate(flops=1, bytes_accessed=4 * tok * d_model, transcendentals=0),
        )(*(pltpu.with_memory_space_constraint(a, pltpu.VMEM) for a in (y, k, v)))

    row_spec = P(('dp', 'cp'), None)
    tok_spec = P(('dp', 'cp'))
    return jax.shard_map(local_block, mesh=mesh,
                         in_specs=(row_spec, tok_spec, P(None, 'tp'), P('tp'), P(None, None), P(None), P('tp', None), P(None), P(None), P(None)),
                         out_specs=(row_spec, row_spec, row_spec), check_vma=False)
```

profile of v0, /device:TPU:3, one launch (start us, length us, event | category | flops | bytes accessed | tf_op | source)
XLA Modules:
  0.0 92.2 jit_solution(900208705263516899)
XLA Ops:
  0.6 89.6 %shard_map.121 = (bf16[256,6144]{1,0:T(8,128)(2,1)S(1)}, bf16[256,128]{1,0:T(8,128)(2,1)S(1)}, bf16[256,128]{1,0:T(8,128)(2,1)S(1)}) custom-call(bf16[256,6144]{1,0:T(8,128)(2,1)} %hid_hbm.1, s32[2,128]{1,0:T(2,128)} %bitcast.10, bf16[6144,3072]{1,0:T(8,128)(2,1)} %wq_hbm.1, bf16[24,128]{1,0:T(8,128)(2,1)} %bitcast.9, bf16[6144,256]{1,0:T(8,128)(2,1)} %wkv_hbm.1, ...), custom_call_target="tpu_custom_call" | custom-call | flops 20132659200 | bytes 150994944 | tf_op jit(solution)/shard_map/pallas_call | solution.py:380
  90.2 1.8 %shard_map.122 = (bf16[256,6144]{1,0:T(8,128)(2,1)}, bf16[256,128]{1,0:T(8,128)(2,1)}, bf16[256,128]{1,0:T(8,128)(2,1)}) custom-call(bf16[256,6144]{1,0:T(8,128)(2,1)S(1)} %get-tuple-element.6.y_ref, bf16[256,128]{1,0:T(8,128)(2,1)S(1)} %get-tuple-element.7.k_ref, bf16[256,128]{1,0:T(8,128)(2,1)S(1)} %get-tuple-element.8.v_ref), custom_call_target="tpu_custom_call" | custom-call | flops 1 | bytes 6291456 | tf_op jit(solution)/shard_map/pallas_call | solution.py:405
where the time goes:
time: 92.3 us; the launch traced here: 92.2 us
  Pallas kernels  91.4 us (99%)
    pallas_call x1, Pallas kernels, local_block(): pl.pallas_call(functools.partial(block_kernel, n_cp), out_shape=(pltpu.VM...  89.6 us

commit v1 on v0

--- a/solution.py
+++ b/solution.py
@@ -284,7 +284,7 @@
             q_next(j)
             return carry
 
-        lag = jnp.where(my < n_cp // 2, 1, 2)
+        lag = jnp.where(my < n_cp // 2, 1, my)
         q_tile(0, 0)
         lax.fori_loop(1, lag, q_tile, 0)
         with jax.named_scope("mask"):

time: 92.3 us -> 92.6 us (level)
  no operation moved by 1% of the time
where the time goes in v1:
time: 92.6 us; the launch traced here: 92.5 us
  Pallas kernels  91.7 us (99%)
    pallas_call x1, Pallas kernels, local_block(): pl.pallas_call(functools.partial(block_kernel, n_cp), out_shape=(pltpu.VM...  90 us

profile of v1, /device:TPU:3, one launch (start us, length us, event | category | flops | bytes accessed | tf_op | source)
XLA Modules:
  0.0 92.5 jit_solution(11997056310823536386)
XLA Ops:
  0.6 90.0 %shard_map.121 = (bf16[256,6144]{1,0:T(8,128)(2,1)S(1)}, bf16[256,128]{1,0:T(8,128)(2,1)S(1)}, bf16[256,128]{1,0:T(8,128)(2,1)S(1)}) custom-call(bf16[256,6144]{1,0:T(8,128)(2,1)} %hid_hbm.1, s32[2,128]{1,0:T(2,128)} %bitcast.10, bf16[6144,3072]{1,0:T(8,128)(2,1)} %wq_hbm.1, bf16[24,128]{1,0:T(8,128)(2,1)} %bitcast.9, bf16[6144,256]{1,0:T(8,128)(2,1)} %wkv_hbm.1, ...), custom_call_target="tpu_custom_call" | custom-call | flops 20132659200 | bytes 150994944 | tf_op jit(solution)/shard_map/pallas_call | solution.py:380
  90.6 1.8 %shard_map.122 = (bf16[256,6144]{1,0:T(8,128)(2,1)}, bf16[256,128]{1,0:T(8,128)(2,1)}, bf16[256,128]{1,0:T(8,128)(2,1)}) custom-call(bf16[256,6144]{1,0:T(8,128)(2,1)S(1)} %get-tuple-element.6.y_ref, bf16[256,128]{1,0:T(8,128)(2,1)S(1)} %get-tuple-element.7.k_ref, bf16[256,128]{1,0:T(8,128)(2,1)S(1)} %get-tuple-element.8.v_ref), custom_call_target="tpu_custom_call" | custom-call | flops 1 | bytes 6291456 | tf_op jit(solution)/shard_map/pallas_call | solution.py:405
